TPU v7x, 32 devices: a whole 2x2x4 slice. The times are simulated.
32 devices in a mesh: dp: 2 (over x), tp: 4 (over z), sp: 4 (over y, core).
Axes of the slice: x: 2, y: 2, z: 4, core: 2. Of those that a mesh axis runs over, the one named last changes fastest.
Arguments:
- hidden: bfloat16 [32768, 2048], P(('dp', 'sp')), parts along dimension 0
- w_query: bfloat16 [2048, 2048], P(None, 'tp')
- w_key: bfloat16 [2048, 2048], P(None, 'tp')
- w_value: bfloat16 [2048, 2048], P(None, 'tp')
- w_out: bfloat16 [2048, 2048], P('tp')
- branch_bias: float32 [4, 8], replicated
Outputs:
- output: bfloat16 [32768, 2048], P(('dp', 'sp'), 'tp'), parts along dimension 0
There are 2 independent parts. A program takes and returns all parts, laid end to end along the dimension named above; an argument that names none is the same for every part.
All inputs are finite; a program needn't handle non-finite values.
Results may differ from a plain program's by a relative error of at most 0.00343.
Values are sent between devices in bfloat16 or wider.
A program may use at most 1 GiB of HBM per device.

v0:
```python
import functools
import math

import jax
import jax.numpy as jnp
from jax import lax
from jax.experimental import pallas as pl
from jax.experimental.pallas import tpu as pltpu
from jax.sharding import PartitionSpec as P

MESH = pl.DeviceIdType.MESH
BF = jnp.bfloat16
F32 = jnp.float32
B, H, M = 256, 512, 2048
KAPPA = math.log2(math.e) / 16
VMEM = 66_900_000
SLOT = (0, 4, 2, 6, 1, 5, 3, 7)
KEY, VAL, QUE = range(3)
HEADS = range(4)
TWO = range(2)
QUARTERS = range(4)
ROWS = range(8)


def nn(a, b):
    return lax.dot_general(a, b, (((1,), (0,)), ((), ())), preferred_element_type=F32)


def nt(a, b):
    return lax.dot_general(a, b, (((1,), (1,)), ((), ())), preferred_element_type=F32)


def params(**kw):
    return pltpu.CompilerParams(vmem_limit_bytes=VMEM, **kw)


def ds(start, size, align=128):
    return pl.ds(pl.multiple_of(start, align), size)


def part(i, size):
    return slice(i * size, i * size + size)


def phase_matrix(transposed):
    r = lax.broadcasted_iota(jnp.int32, (B, B), int(transposed))
    p = lax.broadcasted_iota(jnp.int32, (B, B), int(not transposed))
    k = r // 32
    return (p == (r % 32) * 8 + k // 2 + 4 * (k % 2)).astype(F32).astype(BF)


def unpermute_kernel(y_ref, o_ref, y_s, o_s, load, store):
    pieces = [(s, j) for s in TWO for j in range(4)]

    def get(i):
        s, j = pieces[i]
        return pltpu.make_async_copy(y_ref.at[s, :, pl.ds(j * 64, 64)], y_s.at[i], load.at[i])

    def put(i):
        return pltpu.make_async_copy(o_s.at[i], o_ref.at[pl.ds(i * H, H)], store.at[i])

    for i in ROWS:
        get(i).start()
    pm = phase_matrix(True)
    for i in range(0, 8, 2):
        group = (i, i + 1)
        for k in group:
            get(k).wait()
        for k in group:
            for j in TWO:
                o_s[k, part(j, B), :] = nn(pm, y_s[k, :, part(j, 32), :].reshape(B, H)).astype(BF)
        for k in group:
            put(k).start()
    for i in ROWS:
        put(i).wait()


def unpermute(y):
    anyspec = pl.BlockSpec(memory_space=pl.ANY)
    return pl.pallas_call(
        unpermute_kernel,
        in_specs=[anyspec],
        out_specs=anyspec,
        out_shape=jax.ShapeDtypeStruct((2 * M, H), BF),
        scratch_shapes=[pltpu.VMEM((8, 8, 64, H), BF), pltpu.VMEM((8, H, H), BF), pltpu.SemaphoreType.DMA((8,)), pltpu.SemaphoreType.DMA((8,))],
        compiler_params=params(),
        name='unpermute',
    )(y)


def tile_steps(q, wide, narrow, s_ref, n_ref, done):
    st = {}
    logits, sums = [], []

    def add(name, x):
        st[name] = st[name] + x if name in st else x

    for groups, ref in ((wide, s_ref), (narrow, n_ref)):
        off = 0
        for keys, parts in groups:
            def qk(keys=keys, parts=parts, off=off, ref=ref):
                s = nt(keys(), q() if ref is s_ref else q()[:B])
                o = 0
                for _, n, b in parts:
                    piece = s[o:o + n]
                    ref[pl.ds(off + o, n), :] = piece
                    t = jnp.max(piece, axis=0, keepdims=True) * KAPPA
                    if b is not None:
                        t = t + fit(b, t)
                    if ref is n_ref:
                        t = jnp.concatenate([t, st['top'][:, B:]], axis=1)
                    st['top'] = jnp.maximum(st['top'], t) if 'top' in st else t
                    o += n
            logits.append(qk)
            for v, n, b in parts:
                def sv(v=v, n=n, b=b, off=off, ref=ref):
                    top = st['top'] if ref is s_ref else st['top'][:, :B]
                    e = jnp.exp2(ref[pl.ds(off, n), :] * KAPPA - (top if b is None else top - fit(b, top)))
                    name = 'w' if ref is s_ref else 'n'
                    add('l' + name, jnp.sum(e, axis=0, keepdims=True))
                    add('o' + name, nn(v(), e.astype(BF)))
                sums.append(sv)
                off += n

    def finish():
        o, l = st['ow'], st['lw']
        if narrow:
            o = jnp.concatenate([o[:, :B] + st['on'], o[:, B:]], axis=1)
            l = jnp.concatenate([l[:, :B] + st['ln'], l[:, B:]], axis=1)
        done(o / l)

    return logits, sums + [finish]


def fit(b, like):
    return b if b.shape == like.shape else jnp.concatenate([b] * (like.shape[1] // 128), axis=1)


def interleave(a, b):
    i = j = 0
    while i < len(a) or j < len(b):
        if j >= len(b) or (i < len(a) and i * len(b) <= j * len(a)):
            a[i]()
            i += 1
        else:
            b[j]()
            j += 1


def run_tiles(tiles):
    before = []
    for logits, sums in tiles:
        interleave(logits, before)
        before = sums
    interleave([], before)


def choose(x, cases):
    def among(lo, hi):
        mid = (lo + hi) // 2
        if hi - lo == 1:
            cases[lo]()
        else:
            pl.when(x < mid)(lambda: among(lo, mid))
            pl.when(x >= mid)(lambda: among(mid, hi))
    among(0, len(cases))


def on(cond, *calls):
    @pl.when(cond)
    def _():
        for c in calls:
            c()


def scope(name):
    return jax.named_scope(name)


def main_kernel(bias_ref, x_ref, wk_ref, wv_ref, wq_ref, wout_ref, out_ref, lq_ref, lo_ref, lb_ref,
                xb, pm, xp, ws, q_s, kv_s, kvp_s, kvr_s, s_scr, t_scr,
                beta_s, x_sem, w_sem, wo_sem, sent, lq_recv, lo_recv, lb_recv, kv_recv, o_recv, y_recv, ready):
    dp, tp, sp = lax.axis_index('dp'), lax.axis_index('tp'), lax.axis_index('sp')
    idx = dp * 4 + sp
    side = tp // 2
    inner = (tp == 1) | (tp == 2)
    outer = jnp.logical_not(inner)
    W = (wk_ref, wv_ref, wq_ref)
    peer_x, peer_y, peer_c = {'dp': dp ^ 1}, {'sp': sp ^ 2}, {'sp': sp ^ 1}

    def remote(src, dst, ss, rs, dev):
        return pltpu.make_async_remote_copy(src_ref=src, dst_ref=dst, send_sem=ss, recv_sem=rs, device_id=dev, device_id_type=MESH)

    def lq_copy(t, src, dst, dev):
        return remote(lq_ref.at[src, t], lq_ref.at[dst, t], sent.at[0], lq_recv.at[t, min(dst, 4)], dev)

    def lq_z(t):
        return remote(W[t // 2].at[ds(idx * B, B), pl.ds(t % 2 * B, B)], lq_ref.at[0, t], sent.at[0], lq_recv.at[t, 0], {'tp': tp ^ 2})

    def lq_start(t):
        for i in TWO:
            lq_z(2 * t + i).start()

    def lo_copy(v, src, dst, dev):
        return remote(lo_ref.at[v, src], lo_ref.at[v, dst], sent.at[1], lo_recv.at[v, min(dst, 4)], dev)

    def lo_z(v):
        dst = 2 - side
        b = (tp ^ dst) - 2
        return remote(wout_ref.at[ds(idx * 64, 64, 64), ds((dst ^ v) * H, H)], lo_ref.at[v, 0, b], sent.at[2], lo_recv.at[v, 0], {'tp': dst})

    def lb_z(v):
        return remote(wout_ref.at[ds(sp % 2 * B, B), ds((tp ^ 1 ^ v) * H, H)], lb_ref.at[v, sp % 2], sent.at[3], lb_recv.at[v, 0], {'tp': tp ^ 1})

    def lb_core(v):
        return remote(lb_ref.at[v, sp % 2], lb_ref.at[v, sp % 2], sent.at[3], lb_recv.at[v, 1], peer_c)

    def lo_start(*vs):
        for v in vs:
            lo_z(v).start()

    def arrived(ref, sem):
        remote(ref, ref, sent.at[0], sem, peer_c).wait_recv()

    def all_sent(ref, i):
        remote(ref, ref, sent.at[i], sent.at[i], peer_c).wait_send()

    def lo_zwait(v):
        arrived(lo_ref.at[v, 0], lo_recv.at[v, 0])

    def hop(copy, p, i):
        near, far, n = (peer_x, peer_y, 1) if (copy is lo_copy and p == 2) or (copy is lq_copy and p == 5) else (peer_y, peer_x, 2)
        f = 3 - n
        return copy(p, *((0, n, near), (0, f, far), (0, 4, peer_c), (n, 3, far), (n, 4 + n, peer_c), (f, 4 + f, peer_c), (3, 7, peer_c))[i])

    def ev_z(copy, *ps):
        for p in ps:
            with scope(f'z_{copy.__name__}{p}'):
                lq_z(p).wait_recv() if copy is lq_copy else lo_zwait(p)
            hop(copy, p, 0).start()
        for p in ps:
            hop(copy, p, 1).start()
            hop(copy, p, 2).start()

    def ev_near(copy, *ps):
        for p in ps:
            with scope(f'n_{copy.__name__}{p}'):
                hop(copy, p, 0).wait_recv()
            hop(copy, p, 3).start()
            hop(copy, p, 4).start()

    def ev_far(copy, *ps):
        for p in ps:
            with scope(f'f_{copy.__name__}{p}'):
                hop(copy, p, 1).wait_recv()
            hop(copy, p, 5).start()

    def ev_xy(copy, *ps):
        ev_near(copy, *ps)
        ev_far(copy, *ps)

    def ev_y(copy, *ps):
        for p in ps:
            with scope(f'y_{copy.__name__}{p}'):
                hop(copy, p, 3).wait_recv()
            hop(copy, p, 6).start()
            if copy is lq_copy and p >= 2:
                start(w_load(p, SLOT[:4]))

    def ev_done(copy, *ps):
        for p in ps:
            with scope(f'c_{copy.__name__}{p}'):
                if copy is lq_copy:
                    arrived(lq_ref.at[pl.ds(4, 4), p], lq_recv.at[p, 4])
                else:
                    arrived(lo_ref.at[p, pl.ds(4, 4)], lo_recv.at[p, 4])

    def w_load(p, slots):
        return [pltpu.make_async_copy(lq_ref.at[SLOT.index(m), p], ws.at[p // 2 % 2, ds((idx ^ m) * B, B), pl.ds(p % 2 * B, B)], w_sem.at[p]) for m in slots]

    def own_load(t):
        return pltpu.make_async_copy(W[t], ws.at[t], w_sem.at[6 + t])

    def start(copies):
        for c in copies:
            c.start()

    def wait(copies):
        for c in copies:
            c.wait()

    def ev_last(t):
        pieces = [2 * t + i for i in TWO]
        ev_done(lq_copy, *pieces)
        for p in pieces:
            start(w_load(p, SLOT[4:] if t else SLOT))

    def local(ref, sem):
        pltpu.make_async_copy(ref, ref, sem).wait()

    def ev_weights(t):
        with scope(f'load{t}'):
            for i in TWO:
                local(ws.at[t % 2, :, pl.ds(i * B, B)], w_sem.at[2 * t + i])

    def ev_wo(*vs):
        ev_done(lo_copy, *vs)
        for v in vs:
            lb_core(v).wait_recv()
        start(wo_load(*vs))

    def ev_wo_ready(*vs):
        with scope(f'wo{vs[0]}'):
            for v in vs:
                local(xp.at[1 - side, pl.ds(2, 6), :, pl.ds((v ^ 2) * H, H)], wo_sem.at[v])

    def ev_lb(*vs):
        for v in vs:
            with scope(f'lb{v}'):
                lb_z(v).wait_recv()
            lb_core(v).start()

    wo = xp.at[1 - side]

    def wo_own():
        return [pltpu.make_async_copy(wout_ref.at[pl.ds(r * B, B), pl.ds(c * H, H)], xp.at[1 - side, r, :, ds((c ^ tp ^ 2) * H, H)], wo_sem.at[4])
                for r in TWO for c in range(4)]

    def wo_load(*vs):
        out = []
        for v in vs:
            cols = pl.ds((v ^ 2) * H, H)
            for s, m in enumerate(SLOT):
                row = (idx ^ m) * 64
                for b in TWO:
                    out.append(pltpu.make_async_copy(lo_ref.at[v, s, b], xp.at[1 - side, 4 + 2 * b + row // B, ds(row % B, 64, 64), cols], wo_sem.at[v]))
            for r in TWO:
                out.append(pltpu.make_async_copy(lb_ref.at[v, r], xp.at[1 - side, 2 + r, :, cols], wo_sem.at[v]))
        return out

    def kvp_copy(h, s):
        return remote(kv_s.at[h, pl.ds(8 * s, 2)], kvp_s.at[h, pl.ds(2 * s, 2)], sent.at[4], kv_recv.at[0, h], peer_c)

    def kvr_copy(h, s):
        return remote(kv_s.at[h, 8 * s], kvr_s.at[h, s], sent.at[5], kv_recv.at[1, h], peer_y)

    def kvf_copy(h, s):
        return remote(kvr_s.at[h, s], kvr_s.at[h, 2 + s], sent.at[6], kv_recv.at[2, h], peer_c)

    def kv_start(copy, heads):
        for h in heads:
            for s in TWO:
                copy(h, s).start()

    def kv_wait(copy, heads):
        with scope(f'w_{copy.__name__}{heads[0]}'):
            for h in heads:
                i = (kvp_copy, kvr_copy, kvf_copy).index(copy)
                arrived((kvp_s.at[h], kvr_s.at[h, pl.ds(0, 2)], kvr_s.at[h, pl.ds(2, 2)])[i], kv_recv.at[i, h])

    def kv_forward(heads):
        kv_wait(kvr_copy, heads)
        kv_start(kvf_copy, heads)

    def reverse(i):
        return (i % 2) * 2 + i // 2

    def order(n):
        return 2 * reverse(n % 4) + ((n // 4) ^ side)

    def o_at(k, p, theirs, col, size, row=0, rows=B):
        if p:
            return ws.at[1 + theirs, ds(k * B + row, rows, 64), ds(col, size)]
        return xb.at[k // 2, pl.ds(row, rows), ds((k % 2) * 1024 + theirs * H + col, size)]

    def o_copy(k, p, q):
        row = q * 64
        return remote(o_at(k, p, 0, 0, H, row, 64), o_at(k, p, 1, 0, H, row, 64), sent.at[7], o_recv.at[k, q], {'tp': tp ^ 1})

    def o_times(k, v, n, row=0, rows=B):
        cols = pl.ds((v ^ 2) * H, n * H)
        y = nn(xb[k // 2, pl.ds(row, rows), ds((k % 2) * 1024, 1024)], wo[0:4, :, cols].reshape(1024, n * H))
        for i in TWO:
            y = y + nn(ws[1 + i, ds(k * B + row, rows, 64), :], wo[part(2 + i, 2), :, cols].reshape(H, n * H))
        y = y.astype(BF)
        for i in range(n):
            y_src(k, v + i, row, rows)[...] = y[:, part(i, H)]
            y_copy(k, v + i, side, row, rows).start() if v else y_local(k).start()

    def y_src(k, v, row=0, rows=B):
        return xp.at[side, k, pl.ds(row, rows), pl.ds(v * H, H)]

    def y_copy(k, v, seg, row, rows):
        return remote(y_src(k, v, row, rows), out_ref.at[seg, k, pl.ds(row, rows)], sent.at[8], y_recv.at[seg], {'tp': tp ^ v})

    def y_local(k):
        return pltpu.make_async_copy(y_src(k, 0), out_ref.at[side, k], sent.at[9])

    def x_copy(j):
        return pltpu.make_async_copy(x_ref.at[ds(j * B, B), :], xb.at[lax.rem(j, 4)], x_sem.at[lax.rem(j, 4)])

    for j in range(4):
        x_copy(j).start()
    barrier = pltpu.get_barrier_semaphore()
    peers = [{'tp': tp ^ 1}, {'tp': tp ^ 2}, {'tp': tp ^ 3}, peer_x, peer_y, peer_c]
    for dev in peers:
        pl.semaphore_signal(barrier, inc=1, device_id=dev, device_id_type=MESH)
    for t in range(3):
        own_load(t).start()

    pm[...] = phase_matrix(False)

    def permute_body(j, carry):
        x_copy(j).wait()
        y = nn(pm[...], xb[lax.rem(j, 4)]).astype(BF).reshape(8, 32, M)
        xp[j // 8, :, ds(lax.rem(j, 8) * 32, 32, 32), :] = y
        pl.when(j < 12)(lambda: x_copy(j + 4).start())

        @pl.when(j == 2)
        def _():
            with scope('barrier'):
                pl.semaphore_wait(barrier, len(peers))
            lq_start(KEY)
            on(outer, lb_z(2).start)
        return carry

    with scope('permute'):
        lax.fori_loop(0, 16, permute_body, None)

    for h in HEADS:
        column = 2 * (tp ^ (h // 2 * 2)) + h % 2
        for i, branches in enumerate(('0', '01', '1', '012', '12', '2', '0123', '123', '23', '3')):
            rows = [jnp.full((1, 128), bias_ref[j, column], F32) for j in map(int, branches)]
            m = functools.reduce(jnp.maximum, rows)
            beta_s[pl.ds(h * 16 + i, 1), :] = (m + jnp.log(sum(jnp.exp(r - m) for r in rows))) * math.log2(math.e)

    def signal_ready(i):
        pl.when(inner)(lambda: pl.semaphore_signal(ready.at[i], inc=1, device_id={'tp': tp ^ 1}, device_id_type=MESH))

    def wait_ready(i):
        with scope(f'ready{i}'):
            pl.when(outer)(lambda: pl.semaphore_wait(ready.at[i], 1))

    signal_ready(0)

    def group(g):
        low = g < 4
        return jnp.where(low, g & 1, 0), jnp.where(low, g // 2, g - 2)

    def head_number(h):
        return 2 * (tp ^ (h // 2 * 2)) + h % 2

    def project(heads, sigma, pair, kinds):
        for h in heads:
            t = head_number(h) + reverse(pair)
            x, swap = xp[side ^ sigma, pl.ds(2 * (t & 3), 2)].reshape(H, M), (t & 7) >> 2
            for t in kinds:
                y = nn(x, ws[t, :, part(h % 2, B)])
                for j in TWO:
                    piece = y[part(j, B)]
                    kv_s[h, 8 * sigma + 2 * pair + (j ^ swap), t] = (piece.T if t == VAL else piece).astype(BF)

    def phases_of(j):
        return [j % 2 + 2 * i for i in TWO], (j // 2) ^ side

    def rank_of(phase, h):
        rel = (phase - head_number(h)) & 7
        return (rel & 1) * 4 + ((rel >> 1) & 1) * 2 + (rel >> 2)

    def queries(heads, w, j):
        phases, half = phases_of(j)
        x = jnp.concatenate([xp[side, 2 * f + half] for f in phases])
        for h in heads:
            y = nn(x, ws[w, :, part(h % 2, B)]).astype(BF)
            for i, f in enumerate(phases):
                q_s[h, rank_of(f + 4 * half, h)] = y[part(i, B)]

    with scope('own_w'):
        for t in range(3):
            own_load(t).wait()
    own, partner = HEADS[:2], HEADS[2:]

    def mix(b, c):
        return jnp.concatenate([b, b, c, c], axis=1)

    def keys_of(ref, h, i, weights):
        parts = []
        n = 0
        for count, b in weights:
            def values(i=i + n, count=count):
                v = [ref[h, i + j, VAL] for j in range(count)]
                return v[0] if count == 1 else jnp.concatenate(v, axis=1)
            parts.append((values, count * B, b))
            n += count
        return (lambda: ref[h, i:i + n, KEY].reshape(n * B, B)), parts

    def chunk_tiles(p, j, kind):
        both_phases, half = phases_of(j)

        def put(h, phase, ot):
            k = 2 * (phase & 3) + half
            y = ot.T.astype(BF)
            for i in TWO:
                pl.when(p == i)(lambda i=i: o_at(k, i, 0, (h % 2) * B, B).__setitem__(..., y))

        def tile(h, phases, ranks, wide, narrow, s_ref, n_ref):
            def done(ot):
                for i, phase in enumerate(phases):
                    put(h, phase, ot[:, part(i, B)])
            return tile_steps(lambda: jnp.concatenate([q_s[h, r] for r in ranks]), wide, narrow, s_ref, n_ref, done)

        h = 2 * p + (j % 2) ^ 1
        rest = tile(h, both_phases, [rank_of(f + 4 * half, h) for f in both_phases], [keys_of(kv_s, h, i, [(1, None)]) for i in ROWS], [], t_scr, None)
        h = 2 * p + (j % 2)
        a = head_number(h)
        b0, b01, b1, b012, b12, b2, b0123, b123, b23, b3 = [beta_s[pl.ds(h * 16 + i, 1), :] for i in range(10)]
        phases = [a & 3, (a & 3) ^ 2]
        both = [keys_of(kv_s, h, i, [(2, b)] * n) for i, b, n in ((2, b01, 1), (4, b0, 2), (10, b1, 1))]
        if kind == 0:
            both += [keys_of(kv_s, h, 0, [(1, mix(b0123, b01)), (1, mix(b012, b01))]), keys_of(kv_s, h, 8, [(1, mix(b123, b1)), (1, mix(b12, b1))])]
            first = [keys_of(kvp_s, h, i, [(1, b23), (1, b2)]) for i in (0, 2)] + [keys_of(kvr_s, h, i, [(2, b3)]) for i in (0, 2)]
        else:
            both += [keys_of(kv_s, h, 0, [(2, mix(b012, b01))]), keys_of(kv_s, h, 8, [(2, mix(b12, b1))])]
            first = [keys_of(kvp_s, h, i, [(2, b2)]) for i in (0, 2)]
        with scope(f'tile{kind}'):
            run_tiles([rest, tile(h, phases, [kind, rank_of(phases[1] + 4 * half, h)], both, first, s_scr, t_scr.at[:, pl.ds(0, B)])])

    def send_o(ks, p):
        @pl.when(outer)
        def _():
            for k in ks:
                for q in QUARTERS:
                    o_copy(order(k), p, q).start()

    def step_body(t, carry):
        packed = functools.reduce(lambda x, i: jnp.where(t == i, TABLE[i], x), range(len(TABLE)), 0)
        code, n, event = packed % 16, packed // 16 % 16, packed // 256

        def step_o():
            with scope('own_kv'):
                project(own, *group(n), (KEY, VAL))

        def step_kv(t_):
            with scope(f'par_{t_}'):
                for i in TWO:
                    project(partner, *group(2 * n + i), (t_,))

        def step_q(heads, w):
            with scope(f'que_{w}'):
                queries(heads, w, n)

        def step_out(v, m):
            @pl.when(inner)
            def _():
                k = order(n)

                def wait_for(q):
                    arrived(ws.at[0, pl.ds(0, 128), :], o_recv.at[k, q])

                def quarters():
                    for q in QUARTERS:
                        with scope(f'wait_q{q}'):
                            wait_for(q)
                        o_times(k, v, m, q * 64, 64)
                        if q == 0:
                            ev_y(lo_copy, 1)
                        if q == 2:
                            ev_wo(1)

                def whole():
                    with scope('wait_o'):
                        for q in QUARTERS:
                            wait_for(q)
                    with scope(f'out{v}'):
                        o_times(k, v, m)

                if m == 2:
                    pl.when(n == 0)(quarters)
                    pl.when(n > 0)(whole)
                else:
                    with scope(f'out{v}'):
                        o_times(k, v, m)

        f = functools.partial
        kinds = {'-': lambda: None, 'O': step_o, 'P': f(step_q, own, QUE), 'K': f(step_kv, KEY), 'V': f(step_kv, VAL), 'Q': f(step_q, partner, KEY),
                 'A': lambda: chunk_tiles(n // 4, n % 4, 0), 'B': lambda: chunk_tiles(n // 4, n % 4, 1), 'R': f(step_out, 2, 2), 'L': f(step_out, 1, 1), 'N': f(step_out, 0, 1)}
        choose(code, [kinds[c] for c in KINDS])
        call = functools.partial

        events = {
            'free': [call(signal_ready, 1), call(on, inner, lambda: start(wo_own()))],
            'r0': [call(wait_ready, 0)],
            'r1': [call(wait_ready, 1)],
            'ko': [call(kv_start, kvp_copy, own)],
            'po': [call(kv_wait, kvp_copy, own)],
            'kp': [call(kv_start, kvp_copy, partner)],
            'pp': [call(kv_wait, kvp_copy, partner)],
        }
        for t_, c in enumerate('kvq'):
            events['b' + c] = [call(lq_start, t_)]
            events['l' + c] = [call(ev_last, t_)]
            events['w' + c] = [call(ev_weights, t_)]
            events['z' + c] = [call(ev_z, lq_copy, 2 * t_, 2 * t_ + 1)]
            for i in TWO:
                for e, f in zip('zmfxy', (ev_z, ev_near, ev_far, ev_xy, ev_y)):
                    events[f'{e}{c}{i}'] = [call(f, lq_copy, 2 * t_ + i)]
        for i, vs in enumerate(((2, 3), (1,), (0,))):
            events[f'b{i}'] = [call(lo_start, *vs)]
            for e, f in zip('zmxycwv', (call(ev_z, lo_copy), call(ev_near, lo_copy), call(ev_far, lo_copy), call(ev_y, lo_copy), ev_lb, ev_wo, ev_wo_ready)):
                events[f'{e}{i}'] = [call(on, inner, call(f, *vs))]
        events['v0'] += [call(on, inner, lambda: local(xp.at[1 - side, pl.ds(0, 2)], wo_sem.at[4]))]
        for v in range(4):
            events[f'd{v}'] = [call(on, outer, lambda v=v: lb_z(v).start())]
        for h in HEADS:
            for z in TWO:
                events[f's{h}{z}'] = [kvr_copy(h, z).start]
            events[f'f{h}'] = [call(kv_forward, [h])]
            events[f'g{h}'] = [call(kv_wait, kvf_copy, [h])]
        for k in ROWS:
            for p in TWO:
                events['op'[p] + str(k)] = [call(send_o, (k,), p)]
        def run(names):
            for name in names.split(','):
                where, _, name = name.rpartition(':')
                if where:
                    on(inner if where == 'i' else outer, *events[name])
                else:
                    for c in events[name]:
                        c()

        @pl.when(event > 0)
        def _():
            choose(event - 1, [functools.partial(run, names) for names in EVENTS])
        return carry

    lax.fori_loop(0, len(TABLE), step_body, None)

    all_sent(lq_ref, 0)
    all_sent(lo_ref.at[:, 0, 0], 2)
    all_sent(lb_ref.at[:, 0], 3)
    all_sent(kvp_s, 4)
    all_sent(kvr_s.at[:, pl.ds(0, 2)], 5)
    all_sent(kvr_s.at[:, pl.ds(0, 2)], 6)

    @pl.when(outer)
    def _():
        all_sent(xb, 7)

    @pl.when(inner)
    def _():
        all_sent(lo_ref.at[:, pl.ds(0, 7)], 1)
        with scope('y_sent'):
            all_sent(xp.at[side, :, :, pl.ds(H, 3 * H)], 8)
        local(xp.at[side, :, :, pl.ds(0, H)], sent.at[9])

    for seg in TWO:
        @pl.when(tp != 1 + seg)
        def _(seg=seg):
            with scope(f'recv{seg}'):
                arrived(out_ref.at[seg], y_recv.at[seg])


PROGRAM = (
    'O.i:zk0,i:zk1,bv', 'O.o:zk0', 'O.o:zk1,s00,i:xk0', 'O.o:xk0,i:xk1,o:s01,d3,i:bq', 'O.o:bq,o:xk1,i:yk0,i:zv0', 'O.o:yk0,i:yk1,i:zv1,i:s01',
    'P.o:zv0,o:yk1,lk,o:zv1,d1,i:xv0', 'P.wk,i:xv1', 'K.ko', 'K.o:xv0,i:zq,f0', 'K.o:xv1,i:yv0,i:yv1,b0,b1,r0,po,g0,o:zq',
    'T0.o0,o1,d0,o:yv0,o:yv1,lv,mq0,i:mq1,i:fq0,i:fq1', 'P.wv,o:mq1,b2', 'V.z0,o:fq0,o:fq1,kp,o:s10,o:s11', 'V.c0,z1,o:s20,o:s21,yq0,yq1',
    'V.lq,o:s30,o:s31', 'P.free,wq,m0', 'Q.pp,r1,x0,c1,i:s10,i:s11', 'T4.p0,p1,y0,w0,m1,x1,v0', 'R.v1,i:s20,i:s21', 'L', 'Q.f1', 'R', 'L',
    'T5.p2,g1', 'T1.o2,p3,o3,o:f2', 'R.i:s30,i:s31', 'L', 'Q.o:g2', 'Q.i:f2,o:f3', 'T2', 'R.i:g2', 'L', 'T6.p4,o4,p5,o5,o:g3', 'R.i:f3,z2,c2', 'L',
    'T3.i:g3', 'T7.p6,o6,p7,o7', 'R', 'L.m2,x2', 'R.y2', 'L.w2', '-.v2', 'N', 'N', 'N', 'R', 'L', 'N', 'N', 'N', 'N', 'N',
)
KINDS = '-OPKVQABRLN'


def tables():
    table, seen = [], {}
    names = tuple(dict.fromkeys(s.partition('.')[2] for s in PROGRAM if '.' in s))
    for s in PROGRAM:
        name, _, after = s.partition('.')
        kind, n = name[0], seen.get(name[0], 0)
        seen[kind] = n + 1
        if kind == 'T':
            n = int(name[1:])
            kind = 'AB'[n in (2, 3, 4, 5)]
        table.append(KINDS.index(kind) + 16 * n + 256 * (names.index(after) + 1 if after else 0))
    return table, names


TABLE, EVENTS = tables()


def main(bias, x, wk, wv, wq, w_out):
    anyspec = pl.BlockSpec(memory_space=pl.ANY)
    vmem = [((4, B, M), BF), ((B, B), BF), ((2, 8, B, M), BF), ((3, M, H), BF), ((4, 8, B, B), BF), ((4, 12, 2, B, B), BF), ((4, 4, 2, B, B), BF), ((4, 4, 2, B, B), BF),
            ((3072, H), F32), ((M, H), F32), ((64, 128), F32)]
    dma = [(4,), (9,), (5,), (10,), (6, 5), (4, 5), (4, 2), (3, 4), (8, 4), (2,)]
    return pl.pallas_call(
        main_kernel,
        in_specs=[pl.BlockSpec(memory_space=pltpu.SMEM)] + [anyspec] * 5,
        out_specs=[anyspec] * 4,
        out_shape=[jax.ShapeDtypeStruct(s, BF) for s in ((2, 8, B, H), (8, 6, B, B), (4, 8, 2, 64, H), (4, 2, B, H))],
        scratch_shapes=[pltpu.VMEM(*v) for v in vmem] + [pltpu.SemaphoreType.DMA(d) for d in dma] + [pltpu.SemaphoreType.REGULAR((2,))],
        compiler_params=params(collective_id=0, has_side_effects=True),
        cost_estimate=pl.CostEstimate(flops=10**11, bytes_accessed=10**8, transcendentals=0),
        name='main',
    )(bias, x, wk, wv, wq, w_out)[0]


def solution(mesh):
    def device_fn(hidden, w_query, w_key, w_value, w_out, branch_bias):
        return unpermute(main(branch_bias, hidden, w_key, w_value, w_query, w_out))

    return jax.shard_map(device_fn, mesh=mesh, in_specs=(P(('dp', 'sp'), None), P(None, 'tp'), P(None, 'tp'), P(None, 'tp'), P('tp', None), P(None, None)), out_specs=P(('dp', 'sp'), 'tp'), check_vma=False)
```

profile of v0, /device:TPU:0, one launch (start us, length us, event | category | flops | bytes accessed | tf_op | source)
XLA Modules:
  0.0 170.6 jit_solution(4010438948256737107)
XLA Ops:
  0.0 166.5 %main.1 = (bf16[2,8,256,512]{3,2,1,0:T(8,128)(2,1)}, bf16[8,6,256,256]{3,2,1,0:T(8,128)(2,1)}, bf16[4,8,2,64,512]{4,3,2,1,0:T(8,128)(2,1)}, bf16[4,2,256,512]{3,2,1,0:T(8,128)(2,1)}) custom-call(f32[4,8]{1,0:T(4,128)} %bias_ref.1, bf16[4096,2048]{1,0:T(8,128)(2,1)} %x_ref.1, bf16[2048,512]{1,0:T(8,128)(2,1)} %wk_ref.1, bf16[2048,512]{1,0:T(8,128)(2,1)} %wv_ref.1, ...), custom_call_target="tpu_custom_call" | custom-call | flops 99999997952 | bytes 100000000 | tf_op jit(solution)/shard_map/main/pallas_call | solution.py:696
  166.5 4.1 %unpermute.1 = bf16[4096,512]{1,0:T(8,128)(2,1)} custom-call(bf16[2,8,256,512]{3,2,1,0:T(8,128)(2,1)} %get-tuple-element.6.y_ref), custom_call_target="tpu_custom_call" | custom-call | tf_op jit(solution)/shard_map/unpermute/pallas_call | solution.py:80
where the time goes:
time: 171 us
  Pallas kernels  171 us (100%)
    pallas_call x1, Pallas kernels, main(): pl.pallas_call(main_kernel, in_specs=[pl.BlockSpec(memory_space=pltpu.SME...  166 us
    pallas_call x1, Pallas kernels, unpermute(): pl.pallas_call(unpermute_kernel, in_specs=[anyspec], out_specs=anyspec, o...  4.08 us

commit v1 on v0

--- a/solution.py
+++ b/solution.py
@@ -229,7 +229,7 @@
         arrived(lo_ref.at[v, 0], lo_recv.at[v, 0])
 
     def hop(copy, p, i):
-        near, far, n = (peer_x, peer_y, 1) if (copy is lo_copy and p == 2) or (copy is lq_copy and p == 5) else (peer_y, peer_x, 2)
+        near, far, n = (peer_x, peer_y, 1) if (copy is lo_copy and p == 2) or (copy is lq_copy and p in (3, 5)) else (peer_y, peer_x, 2)
         f = 3 - n
         return copy(p, *((0, n, near), (0, f, far), (0, 4, peer_c), (n, 3, far), (n, 4 + n, peer_c), (f, 4 + f, peer_c), (3, 7, peer_c))[i])
 
@@ -662,8 +662,8 @@
 
 PROGRAM = (
     'O.i:zk0,i:zk1,bv', 'O.o:zk0', 'O.o:zk1,s00,i:xk0', 'O.o:xk0,i:xk1,o:s01,d3,i:bq', 'O.o:bq,o:xk1,i:yk0,i:zv0', 'O.o:yk0,i:yk1,i:zv1,i:s01',
-    'P.o:zv0,o:yk1,lk,o:zv1,d1,i:xv0', 'P.wk,i:xv1', 'K.ko', 'K.o:xv0,i:zq,f0', 'K.o:xv1,i:yv0,i:yv1,b0,b1,r0,po,g0,o:zq',
-    'T0.o0,o1,d0,o:yv0,o:yv1,lv,mq0,i:mq1,i:fq0,i:fq1', 'P.wv,o:mq1,b2', 'V.z0,o:fq0,o:fq1,kp,o:s10,o:s11', 'V.c0,z1,o:s20,o:s21,yq0,yq1',
+    'P.o:zv0,o:yk1,lk,o:zv1,d1,i:xv0', 'P.wk,i:xv1', 'K.ko', 'K.o:xv1,o:xv0,i:zq,f0', 'K.i:yv0,i:yv1,b0,b1,r0,po,g0,o:zq',
+    'T0.o0,o1,d0,o:yv0,o:yv1,lv,i:mq0,i:mq1,i:fq0,i:fq1', 'P.wv,o:mq0,o:mq1,b2', 'V.z0,o:fq0,o:fq1,kp,o:s10,o:s11', 'V.c0,z1,o:s20,o:s21,yq0,yq1',
     'V.lq,o:s30,o:s31', 'P.free,wq,m0', 'Q.pp,r1,x0,c1,i:s10,i:s11', 'T4.p0,p1,y0,w0,m1,x1,v0', 'R.v1,i:s20,i:s21', 'L', 'Q.f1', 'R', 'L',
     'T5.p2,g1', 'T1.o2,p3,o3,o:f2', 'R.i:s30,i:s31', 'L', 'Q.o:g2', 'Q.i:f2,o:f3', 'T2', 'R.i:g2', 'L', 'T6.p4,o4,p5,o5,o:g3', 'R.i:f3,z2,c2', 'L',
     'T3.i:g3', 'T7.p6,o6,p7,o7', 'R', 'L.m2,x2', 'R.y2', 'L.w2', '-.v2', 'N', 'N', 'N', 'R', 'L', 'N', 'N', 'N', 'N', 'N',

time: 171 us -> 173 us (1.012)
  Pallas kernels: 171 us -> 173 us
    pallas_call x1, Pallas kernels: 166 us -> 169 us  [main(): pl.pallas_call(main_kernel, in_specs=[pl.BlockSpec(memory_space=pltpu.SME...]
where the time goes in v1:
time: 173 us
  Pallas kernels  173 us (100%)
    pallas_call x1, Pallas kernels, main(): pl.pallas_call(main_kernel, in_specs=[pl.BlockSpec(memory_space=pltpu.SME...  169 us
    pallas_call x1, Pallas kernels, unpermute(): pl.pallas_call(unpermute_kernel, in_specs=[anyspec], out_specs=anyspec, o...  4.07 us

profile of v1, /device:TPU:0, one launch (start us, length us, event | category | flops | bytes accessed | tf_op | source)
XLA Modules:
  0.0 172.8 jit_solution(14595972790103093695)
XLA Ops:
  0.0 168.8 %main.1 = (bf16[2,8,256,512]{3,2,1,0:T(8,128)(2,1)}, bf16[8,6,256,256]{3,2,1,0:T(8,128)(2,1)}, bf16[4,8,2,64,512]{4,3,2,1,0:T(8,128)(2,1)}, bf16[4,2,256,512]{3,2,1,0:T(8,128)(2,1)}) custom-call(f32[4,8]{1,0:T(4,128)} %bias_ref.1, bf16[4096,2048]{1,0:T(8,128)(2,1)} %x_ref.1, bf16[2048,512]{1,0:T(8,128)(2,1)} %wk_ref.1, bf16[2048,512]{1,0:T(8,128)(2,1)} %wv_ref.1, ...), custom_call_target="tpu_custom_call" | custom-call | flops 99999997952 | bytes 100000000 | tf_op jit(solution)/shard_map/main/pallas_call | solution.py:696
  168.8 4.1 %unpermute.1 = bf16[4096,512]{1,0:T(8,128)(2,1)} custom-call(bf16[2,8,256,512]{3,2,1,0:T(8,128)(2,1)} %get-tuple-element.6.y_ref), custom_call_target="tpu_custom_call" | custom-call | tf_op jit(solution)/shard_map/unpermute/pallas_call | solution.py:80

commit v2 on v0

--- a/solution.py
+++ b/solution.py
@@ -62,8 +62,8 @@
     for i in ROWS:
         get(i).start()
     pm = phase_matrix(True)
-    for i in range(0, 8, 2):
-        group = (i, i + 1)
+    for first, last in ((0, 1), (1, 3), (3, 5), (5, 7), (7, 8)):
+        group = range(first, last)
         for k in group:
             get(k).wait()
         for k in group:

time: 171 us -> 171 us (level)
  no operation moved by 1% of the time
where the time goes in v2:
time: 171 us; the launch traced here: 170 us
  Pallas kernels  170 us (99%)
    pallas_call x1, Pallas kernels, main(): pl.pallas_call(main_kernel, in_specs=[pl.BlockSpec(memory_space=pltpu.SME...  166 us
    pallas_call x1, Pallas kernels, unpermute(): pl.pallas_call(unpermute_kernel, in_specs=[anyspec], out_specs=anyspec, o...  3.96 us

profile of v2, /device:TPU:0, one launch (start us, length us, event | category | flops | bytes accessed | tf_op | source)
XLA Modules:
  0.0 170.5 jit_solution(17948826127262976703)
XLA Ops:
  0.0 166.5 %main.1 = (bf16[2,8,256,512]{3,2,1,0:T(8,128)(2,1)}, bf16[8,6,256,256]{3,2,1,0:T(8,128)(2,1)}, bf16[4,8,2,64,512]{4,3,2,1,0:T(8,128)(2,1)}, bf16[4,2,256,512]{3,2,1,0:T(8,128)(2,1)}) custom-call(f32[4,8]{1,0:T(4,128)} %bias_ref.1, bf16[4096,2048]{1,0:T(8,128)(2,1)} %x_ref.1, bf16[2048,512]{1,0:T(8,128)(2,1)} %wk_ref.1, bf16[2048,512]{1,0:T(8,128)(2,1)} %wv_ref.1, ...), custom_call_target="tpu_custom_call" | custom-call | flops 99999997952 | bytes 100000000 | tf_op jit(solution)/shard_map/main/pallas_call | solution.py:696
  166.5 4.0 %unpermute.1 = bf16[4096,512]{1,0:T(8,128)(2,1)} custom-call(bf16[2,8,256,512]{3,2,1,0:T(8,128)(2,1)} %get-tuple-element.6.y_ref), custom_call_target="tpu_custom_call" | custom-call | tf_op jit(solution)/shard_map/unpermute/pallas_call | solution.py:80
